TPU v7x, 128 devices: a whole 4x4x4 slice. The times are simulated.
128 devices in a mesh: fit: 8 (over z, core), pair: 16 (over x, y).
Axes of the slice: x: 4, y: 4, z: 4, core: 2. Of those that a mesh axis runs over, the one named last changes fastest.
Arguments:
- metric_factor: bfloat16 [4096, 4096], P('fit'), as said below
- three_index: bfloat16 [4096, 32768], P('fit', 'pair'), may hold values from -6 to 6
- send_map: int32 [16, 16, 8], P('pair'), may hold values from 0 to 15
- pair_slots: int32 [16, 128], P('pair'), may hold values from 0 to 127, each once within a row
- pair_count: int32 [16], P('pair'), may hold values from 1 to 64, 512 in all
- orbital_energy: bfloat16 [256], P('pair'), may hold values from -2 to -0.19921875
- cabs_energy: float32 [1024], replicated, may hold values from 0.5 to 4
- coupling: bfloat16 [128, 1024], replicated, may hold values from -0.5 to 0.5
Outputs:
- projected: bfloat16 [16, 64, 128, 1024], P('pair', 'fit')
Inputs may be any that keep to these rules, and one draw needn't show every extreme that they name: `metric_factor`: diagonal entries lie between 0.6 and 1.4. `pair_slots`: each row holds every position 0 to 127 once; pair n of a row uses entries 2n and 2n + 1.
All inputs are finite; a program needn't handle non-finite values. No bound on the sum of `pair_count` on one device may be relied on, other than what follows from the above.
Results may differ from a plain program's by a relative error of at most 0.015.
Values may be sent and summed in bfloat16 or wider, within the bound.
A program may use at most 256 MiB of HBM per device.

v0:
```python
import jax
import jax.numpy as jnp
from jax import lax
from jax.sharding import PartitionSpec as P

NAUX = 4096
PAIR_BLOCK = 8


def turned_gather(arrays, axis, dims):
    turned = [jnp.moveaxis(a, dim, 0) for a, dim in zip(arrays, dims)]
    both = jnp.concatenate([t.reshape(len(t), -1) for t in turned], axis=1)
    filled, at, outs = (lax.all_gather(both, axis, axis=0, tiled=True), 0, [])
    for t, dim in zip(turned, dims):
        slab = filled[:, at : at + t[0].size].reshape(-1, *t.shape[1:])
        outs.append(jnp.moveaxis(slab, 0, dim))
        at += t[0].size
    return tuple(outs)


def on_device(
    metric_factor,
    three_index,
    send_map,
    pair_slots,
    pair_count,
    orbital_energy,
    cabs_energy,
    coupling,
):
    domain = coupling.shape[0]
    orbitals = orbital_energy.shape[0]
    local_rows = metric_factor.shape[0]
    peers = send_map.shape[1]
    capacity = send_map.shape[2]
    slot_total = pair_slots.shape[1] // 2
    fitted = jnp.dot(
        metric_factor,
        lax.all_gather(three_index, "fit", axis=0, tiled=True),
        preferred_element_type=jnp.float32,
    )
    fitted = fitted.astype(jnp.bfloat16).reshape(local_rows, orbitals, domain)
    requests = send_map.reshape(peers, capacity)
    source, energy_src = turned_gather((fitted, orbital_energy), "pair", (1, 0))
    global_ids = (jnp.arange(peers, dtype=jnp.int32)[:, None] * orbitals + requests).reshape(-1)
    pair_index = jnp.take(global_ids, pair_slots[0])
    left_index = pair_index[0::2]
    right_index = pair_index[1::2]
    live_count = pair_count[0]
    norm_scale = NAUX ** (-0.5)
    block_count = (live_count + PAIR_BLOCK - 1) // PAIR_BLOCK

    def advance(block, partial_value):
        left_ids = lax.dynamic_slice_in_dim(left_index, block * PAIR_BLOCK, PAIR_BLOCK)
        right_ids = lax.dynamic_slice_in_dim(right_index, block * PAIR_BLOCK, PAIR_BLOCK)
        left_rows = jnp.take(source, left_ids, axis=1)
        right_rows = jnp.take(source, right_ids, axis=1)
        product = jnp.einsum(
            "qsa,qsb->sab", left_rows, right_rows, preferred_element_type=jnp.float32
        )
        return lax.dynamic_update_slice_in_dim(
            partial_value, product * norm_scale, block * PAIR_BLOCK, 0
        )

    partial_value = jnp.zeros((slot_total, domain, domain), jnp.float32)
    partial_value = lax.fori_loop(0, block_count, advance, partial_value)
    share = slot_total // lax.axis_size("fit")
    first_slot = lax.axis_index("fit") * share
    exchange = lax.psum_scatter(
        partial_value.astype(jnp.bfloat16), "fit", scatter_dimension=0, tiled=True
    )
    energy_sum = jnp.take(energy_src, left_index).astype(jnp.float32) + jnp.take(
        energy_src, right_index
    ).astype(jnp.float32)
    energy_sum = lax.dynamic_slice_in_dim(energy_sum, first_slot, share, 0)
    weighted = jnp.einsum("sab,bc->sac", exchange, coupling, preferred_element_type=jnp.float32)
    denom = cabs_energy[None, None, :] - energy_sum[:, None, None]
    live_mask = first_slot + jnp.arange(share, dtype=jnp.int32) < live_count
    projected = jnp.where(live_mask[:, None, None], weighted / denom, 0.0).astype(jnp.bfloat16)
    return projected.reshape(1, share, domain, weighted.shape[2])


def solution(mesh):
    in_specs = (
        P("fit", None),
        P("fit", "pair"),
        P("pair", None, None),
        P("pair", None),
        P("pair"),
        P("pair"),
        P(),
        P(),
    )
    out_specs = P("pair", "fit", None, None)
    return jax.shard_map(
        on_device, mesh=mesh, in_specs=in_specs, out_specs=out_specs, check_vma=False
    )
```

profile of v0, /device:TPU:0, one launch (start us, length us, event | category | flops | bytes accessed | tf_op | source)
XLA Modules:
  0.0 506.7 jit_solution(18273993454955358155)
XLA Ops:
  6.5 0.7 all-gather.3.cloned.1.call-update
  7.3 0.7 copy.16
  8.1 88.6 %all-gather.3.cloned.1.call-done = bf16[4096,2048]{1,0:T(8,128)(2,1)} async-done(((bf16[512,2048]{1,0:T(8,128)(2,1)}), bf16[4096,2048]{1,0:T(8,128)(2,1)}) %all-gather.3.cloned.1.call-update) | async-done | bytes 16777232 | tf_op jit(solution)/shard_map/all_gather | solution.py:39
  96.7 13.6 %fusion.9 = bf16[64,16,8,128]{3,2,1,0:T(8,128)(2,1)S(1)} fusion(bf16[512,4096]{1,0:T(8,128)(2,1)} %param.14, bf16[4096,2048]{1,0:T(8,128)(2,1)} %all-gather.3.cloned.1.call-done), kind=kOutput, calls=%fused_computation.26 | convolution fusion | flops 8590983168 | bytes 23068672 | tf_op jit(solution)/shard_map/dot_general | solution.py:37
  110.3 0.5 copy.25
  110.8 1.4 copy.24
  112.2 1.5 pad_maximum_fusion
  114.5 0.1 add.77
  114.7 0.1 reshape.106
  114.8 1.2 gather_fusion.2
  116.0 0.2 slice.14
  116.2 0.2 slice.12
  116.4 195.1 %all-gather.5.cloned.1.call-done = bf16[256,65537]{1,0:T(8,128)(2,1)} async-done(((bf16[16,65537]{1,0:T(8,128)(2,1)}), bf16[256,65537]{1,0:T(8,128)(2,1)}) %all-gather.5.cloned.1.call-update) | async-done | bytes 33554960 | tf_op jit(solution)/shard_map/all_gather | solution.py:13
  311.5 22.9 %slice.26 = bf16[256,65536]{1,0:T(8,128)(2,1)} slice(bf16[256,65537]{1,0:T(8,128)(2,1)} %all-gather.5.cloned.1.call-done), slice={[0:256], [0:65536]} | slice | bytes 67108864 | tf_op jit(solution)/shard_map/slice | solution.py:15
  334.3 41.6 %copy.17 = bf16[256,65536]{0,1:T(8,128)(2,1)} copy(bf16[256,65536]{1,0:T(8,128)(2,1)} %slice.26) | data formatting | bytes 67108864 | tf_op jit(solution)/shard_map/slice | solution.py:15
  375.9 43.8 %copy.18 = bf16[512,256,128]{2,0,1:T(8,128)(2,1)} copy(bf16[512,256,128]{1,2,0:T(8,128)(2,1)} %bitcast.41) | data formatting | bytes 67108864 | tf_op jit(solution)/shard_map/while | solution.py:66
  419.7 1.8 broadcast_in_dim.41
  421.5 42.6 %while.10 = (s32[]{:T(128)}, bf16[64,128,128]{2,1,0:T(8,128)(2,1)}, s32[]{:T(128)}, s32[64]{0:T(128)S(1)}, bf16[512,256,128]{2,0,1:T(8,128)(2,1)}, /*index=5*/s3...) while((s32[]{:T(128)}, bf16[64,128,128]{2,1,0:T(8,128)(2,1)}, s32[]{:T(128)}, s32[64]{0:T(128)S(1)}, ...), condition=%wide.region_1.3_spmd, body=%wide.region_0.0_spmd.sunk | while | flops 135399520 | bytes 6824379 | solution.py:66
  421.6 2.0 gather_fusion.1
  423.6 2.0 gather_fusion
  425.5 1.3 fusion.21
  426.9 2.0 gather_fusion.1
  428.9 2.0 gather_fusion
  430.9 1.3 fusion.21
  432.2 2.0 gather_fusion.1
  434.2 2.0 gather_fusion
  436.2 1.3 fusion.21
  437.6 2.0 gather_fusion.1
  439.5 2.0 gather_fusion
  441.5 1.3 fusion.21
  442.9 2.0 gather_fusion.1
  444.9 2.0 gather_fusion
  446.8 1.3 fusion.21
  448.2 2.0 gather_fusion.1
  450.2 2.0 gather_fusion
  452.1 1.3 fusion.21
  453.4 0.1 compare_and_fusion.3
  453.5 2.0 gather_fusion.1
  455.5 2.0 gather_fusion
  457.5 1.3 fusion.21
  458.9 2.0 gather_fusion.1
  460.8 2.0 gather_fusion
  462.8 1.3 fusion.21
  464.2 0.9 slice_reduce_fusion
  465.1 0.8 gather_fusion.4
  465.9 0.8 gather_fusion.3
  466.8 30.3 %reduce-scatter.2.cloned.1.call-done = bf16[8,128,128]{2,1,0:T(8,128)(2,1)} async-done(((bf16[64,128,128]{2,1,0:T(8,128)(2,1)}), bf16[8,128,128]{2,1,0:T(8,128)(2,1)}) %reduce-scatter.2.cloned.1.call-update) | async-done | bytes 262160 | tf_op jit(solution)/shard_map/reduce_scatter | solution.py:69
  497.2 3.0 fusion.10
  (51 shorter events, 1.1 us)
Async XLA Ops:
  6.5 490.6 %copy-start = (bf16[128,1024]{1,0:T(8,128)(2,1)S(1)}, bf16[128,1024]{1,0:T(8,128)(2,1)}, u32[]{:S(2)}) copy-start(bf16[128,1024]{1,0:T(8,128)(2,1)} %param.21) | copy-start | bytes 786436
  6.5 90.1 %all-gather.3.cloned.1.call-start = ((), (), s32[]{:S(2)}) async-start(), calls=%async_computation.1 | async-start | bytes 18874368 | tf_op jit(solution)/shard_map/all_gather | solution.py:39
  7.3 304.2 %all-gather.5.cloned.1.call-start = ((), (), s32[]{:S(2)}) async-start(), calls=%async_computation.2 | async-start | bytes 35721216 | tf_op jit(solution)/shard_map/all_gather | solution.py:13
  112.2 2.4 copy-start.1
  112.2 2.6 copy-start.3
  113.7 383.5 %reduce-scatter.2.cloned.1.call-start = ((), (), s32[]{:S(2)}) async-start(), calls=%async_computation.3 | async-start | bytes 2359296 | tf_op jit(solution)/shard_map/reduce_scatter | solution.py:69
  421.5 45.3 %copy-start.2 = (f32[1024]{0:T(1024)S(1)}, f32[1024]{0:T(1024)}, u32[]{:S(2)}) copy-start(f32[1024]{0:T(1024)} %param.20) | copy-start | bytes 12292
Sparse Core Ops, SparseCore 0:
  9.0 87.5 all-gather.2
  113.8 197.6 all-gather.4
  464.2 32.9 reduce-scatter.1
where the time goes:
time: 509 us; the launch traced here: 507 us
  waiting for transfers between devices  315 us (62%)
  local copies, waits for them, and re-layouts  149 us (29%)
  matrix products  26.9 us (5%)
  between operations  13.9 us (3%)
    all_gather x1, waiting for transfers between devices, turned_gather(): filled, at, outs = (lax.all_gather(both, axis, axis=0, tiled=True), 0, [])  195 us
    all_gather x1, waiting for transfers between devices, on_device(): lax.all_gather(three_index, 'fit', axis=0, tiled=True)  88.6 us
    slice x3, local copies, waits for them, and re-layouts, turned_gather(): slab = filled[:, at:at + t[0].size].reshape(-1, *t.shape[1:])  65.4 us
    while x1, local copies, waits for them, and re-layouts, on_device(): partial_value = lax.fori_loop(0, block_count, advance, partial_value)  43.8 us
    reduce_scatter x1, waiting for transfers between devices, on_device(): lax.psum_scatter(partial_value.astype(jnp.bfloat16), 'fit', scatter_dimen...  30.3 us
    gather x8, local copies, waits for them, and re-layouts, advance(): left_rows = jnp.take(source, left_ids, axis=1)  15.7 us
    gather x8, local copies, waits for them, and re-layouts, advance(): right_rows = jnp.take(source, right_ids, axis=1)  15.7 us
    dot_general x1, matrix products, on_device(): jnp.dot(metric_factor, lax.all_gather(three_index, 'fit', axis=0, tiled=T...  13.6 us
  transfers between devices with their start and end apart: 3, of which 3 were waited for; matrix products, arithmetic and copies ran while one was open for 1% of the time, Pallas kernels for 0%

commit v1 on v0

--- a/solution.py
+++ b/solution.py
@@ -7,10 +7,17 @@
 PAIR_BLOCK = 8
 
 
+def swapped_in(x, mesh_axis, dim):
+    size = lax.axis_size(mesh_axis)
+    pieces = jnp.stack([x for _ in range(size)])
+    pieces = lax.all_to_all(pieces, mesh_axis, split_axis=0, concat_axis=0)
+    return jnp.concatenate(pieces, axis=dim)
+
+
 def turned_gather(arrays, axis, dims):
     turned = [jnp.moveaxis(a, dim, 0) for a, dim in zip(arrays, dims)]
     both = jnp.concatenate([t.reshape(len(t), -1) for t in turned], axis=1)
-    filled, at, outs = (lax.all_gather(both, axis, axis=0, tiled=True), 0, [])
+    filled, at, outs = (swapped_in(both, axis, 0), 0, [])
     for t, dim in zip(turned, dims):
         slab = filled[:, at : at + t[0].size].reshape(-1, *t.shape[1:])
         outs.append(jnp.moveaxis(slab, 0, dim))

time: 509 us -> 953 us (1.87)
  waiting for transfers between devices: 315 us -> 740 us
  local copies, waits for them, and re-layouts: 149 us -> 161 us
    all_to_all x0 -> x1, waiting for transfers between devices: none -> 623 us  [swapped_in(): pieces = lax.all_to_all(pieces, mesh_axis, split_axis=0, concat_axis=0)]
    all_gather x1 -> x0, waiting for transfers between devices: 195 us -> none  [turned_gather(): filled, at, outs = (lax.all_gather(both, axis, axis=0, tiled=True), 0, [])]
    another operation x0 -> x1, local copies, waits for them, and re-layouts: none -> 11 us  [swapped_in(): pieces = jnp.stack([x for _ in range(size)])]
where the time goes in v1:
time: 953 us; the launch traced here: 950 us
  waiting for transfers between devices  740 us (78%)
  local copies, waits for them, and re-layouts  161 us (17%)
  matrix products  26.9 us (3%)
  between operations  14.2 us (1%)
    all_to_all x1, waiting for transfers between devices, swapped_in(): pieces = lax.all_to_all(pieces, mesh_axis, split_axis=0, concat_axis=0)  623 us
    all_gather x1, waiting for transfers between devices, on_device(): lax.all_gather(three_index, 'fit', axis=0, tiled=True)  88.7 us
    slice x3, local copies, waits for them, and re-layouts, turned_gather(): slab = filled[:, at:at + t[0].size].reshape(-1, *t.shape[1:])  67.7 us
    while x1, local copies, waits for them, and re-layouts, on_device(): partial_value = lax.fori_loop(0, block_count, advance, partial_value)  43.1 us
    reduce_scatter x1, waiting for transfers between devices, on_device(): lax.psum_scatter(partial_value.astype(jnp.bfloat16), 'fit', scatter_dimen...  27 us
  transfers between devices with their start and end apart: 3, of which 3 were waited for; matrix products, arithmetic and copies ran while one was open for 1% of the time, Pallas kernels for 0%

profile of v1, /device:TPU:0, one launch (start us, length us, event | category | flops | bytes accessed | tf_op | source)
XLA Modules:
  0.0 950.3 jit_solution(11009331376860748284)
XLA Ops:
  6.5 0.7 all-gather.2.cloned.1.call-update
  7.3 0.7 copy.22
  8.0 88.7 %all-gather.2.cloned.1.call-done = bf16[4096,2048]{1,0:T(8,128)(2,1)} async-done(((bf16[512,2048]{1,0:T(8,128)(2,1)}), bf16[4096,2048]{1,0:T(8,128)(2,1)}) %all-gather.2.cloned.1.call-update) | async-done | bytes 16777232 | tf_op jit(solution)/shard_map/all_gather | solution.py:46
  96.7 13.6 %fusion.9 = bf16[64,16,8,128]{3,2,1,0:T(8,128)(2,1)S(1)} fusion(bf16[512,4096]{1,0:T(8,128)(2,1)} %param.14, bf16[4096,2048]{1,0:T(8,128)(2,1)} %all-gather.2.cloned.1.call-done), kind=kOutput, calls=%fused_computation.26 | convolution fusion | flops 8590983168 | bytes 23068672 | tf_op jit(solution)/shard_map/dot_general | solution.py:44
  110.3 0.5 copy.31
  110.8 1.4 copy.30
  112.2 0.1 pad_maximum_fusion
  112.3 11.0 %stack.2 = bf16[16,16,65537]{2,1,0:T(8,128)(2,1)} broadcast(bf16[16,65537]{1,0:T(8,128)(2,1)S(1)} %pad_maximum_fusion), dimensions={1,2} | broadcast | bytes 35652128 | tf_op jit(solution)/shard_map/stack | solution.py:12
  123.4 7.0 all-to-all-start
  130.5 0.1 add.77
  130.8 1.2 gather_fusion.2
  132.0 0.2 slice.12
  132.2 0.2 slice.14
  133.0 623.4 %all-to-all-done = bf16[16,16,65537]{2,1,0:T(8,128)(2,1)} async-done(((bf16[16,16,65537]{2,1,0:T(8,128)(2,1)}), bf16[16,16,65537]{2,1,0:T(8,128)(2,1)}, u32[]{:S(2)}, u32[]{:S(2)}) %all-to-all-start) | async-done | bytes 33554976 | tf_op jit(solution)/shard_map/all_to_all | solution.py:13
  756.4 22.8 %slice.26 = bf16[256,65536]{1,0:T(8,128)(2,1)} slice(bf16[256,65537]{1,0:T(8,128)(2,1)} %bitcast.8), slice={[0:256], [0:65536]} | slice | bytes 67108864 | tf_op jit(solution)/shard_map/slice | solution.py:22
  779.2 43.9 %copy.23 = bf16[256,65536]{0,1:T(8,128)(2,1)} copy(bf16[256,65536]{1,0:T(8,128)(2,1)} %slice.26) | data formatting | bytes 67108864 | tf_op jit(solution)/shard_map/slice | solution.py:22
  823.1 43.1 %copy.24 = bf16[512,256,128]{2,0,1:T(8,128)(2,1)} copy(bf16[512,256,128]{1,2,0:T(8,128)(2,1)} %bitcast.42) | data formatting | bytes 67108864 | tf_op jit(solution)/shard_map/while | solution.py:73
  866.3 1.8 broadcast_in_dim.41
  868.1 42.6 %while.10 = (s32[]{:T(128)}, bf16[64,128,128]{2,1,0:T(8,128)(2,1)}, s32[]{:T(128)}, s32[64]{0:T(128)S(1)}, bf16[512,256,128]{2,0,1:T(8,128)(2,1)}, /*index=5*/s3...) while((s32[]{:T(128)}, bf16[64,128,128]{2,1,0:T(8,128)(2,1)}, s32[]{:T(128)}, s32[64]{0:T(128)S(1)}, ...), condition=%wide.region_1.3_spmd, body=%wide.region_0.0_spmd.sunk | while | flops 135399520 | bytes 6824387 | solution.py:73
  868.2 2.0 gather_fusion
  870.2 2.0 gather_fusion.1
  872.1 1.3 fusion.21
  873.5 2.0 gather_fusion
  875.5 2.0 gather_fusion.1
  877.5 1.3 fusion.21
  878.8 2.0 gather_fusion
  880.8 2.0 gather_fusion.1
  882.8 1.3 fusion.21
  884.1 2.0 gather_fusion
  886.1 2.0 gather_fusion.1
  888.1 1.3 fusion.21
  889.5 2.0 gather_fusion
  891.4 2.0 gather_fusion.1
  893.4 1.3 fusion.21
  894.8 2.0 gather_fusion
  896.8 2.0 gather_fusion.1
  898.7 1.3 fusion.21
  900.1 2.0 gather_fusion
  902.1 2.0 gather_fusion.1
  904.1 1.3 fusion.21
  905.4 2.0 gather_fusion
  907.4 2.0 gather_fusion.1
  909.4 1.3 fusion.21
  910.8 0.9 slice_reduce_fusion
  911.7 0.8 gather_fusion.3
  912.5 0.8 gather_fusion.4
  913.4 27.0 %reduce-scatter.2.cloned.1.call-done = bf16[8,128,128]{2,1,0:T(8,128)(2,1)} async-done(((bf16[64,128,128]{2,1,0:T(8,128)(2,1)}), bf16[8,128,128]{2,1,0:T(8,128)(2,1)}) %reduce-scatter.2.cloned.1.call-update) | async-done | bytes 262160 | tf_op jit(solution)/shard_map/reduce_scatter | solution.py:76
  940.5 3.0 fusion.10
  (51 shorter events, 1.2 us)
Async XLA Ops:
  6.5 934.0 %copy-start = (bf16[128,1024]{1,0:T(8,128)(2,1)S(1)}, bf16[128,1024]{1,0:T(8,128)(2,1)}, u32[]{:S(2)}) copy-start(bf16[128,1024]{1,0:T(8,128)(2,1)} %param.21) | copy-start | bytes 786436
  6.5 90.1 %all-gather.2.cloned.1.call-start = ((), (), s32[]{:S(2)}) async-start(), calls=%async_computation.2 | async-start | bytes 18874368 | tf_op jit(solution)/shard_map/all_gather | solution.py:46
  123.3 7.2 copy-start.1
  123.3 7.4 copy-start.3
  123.4 633.0 %all-to-all-start = ((bf16[16,16,65537]{2,1,0:T(8,128)(2,1)}), bf16[16,16,65537]{2,1,0:T(8,128)(2,1)}, u32[]{:S(2)}, u32[]{:S(2)}) async-start(bf16[16,16,65537]{2,1,0:T(8,128)(2,1)} %stack.2), calls=%async_computation | async-start | bytes 67239936 | tf_op jit(solution)/shard_map/all_to_all | solution.py:13
  130.3 810.1 %reduce-scatter.2.cloned.1.call-start = ((), (), s32[]{:S(2)}) async-start(), calls=%async_computation.3 | async-start | bytes 2359296 | tf_op jit(solution)/shard_map/reduce_scatter | solution.py:76
  868.1 45.3 %copy-start.2 = (f32[1024]{0:T(1024)S(1)}, f32[1024]{0:T(1024)}, u32[]{:S(2)}) copy-start(f32[1024]{0:T(1024)} %param.20) | copy-start | bytes 12292
Sparse Core Ops, SparseCore 0:
  9.0 87.5 all-gather.1
  910.8 29.6 reduce-scatter.1
